TPU v7x, 512 devices: a whole 4x4x16 slice. The times are simulated.
512 devices in a mesh: dp: 32 (over z_lo, y, core), blk: 16 (over x, z_hi).
Axes of the slice: x: 4, y: 4, z: 16 (z_hi: 4, z_lo: 4; z = z_hi * 4 + z_lo), core: 2. Of those that a mesh axis runs over, the one named last changes fastest.
Arguments:
- block_input_rows: bfloat16 [9216, 16384], P('dp', 'blk'), may hold values from -6 to 6
- up_loss_gradient: bfloat16 [9216, 53248], P('dp', 'blk'), may hold values from -6 to 6
- down_projection_input: bfloat16 [9216, 53248], P('dp', 'blk'), may hold values from -6 to 6
- output_loss_gradient: bfloat16 [9216, 16384], P('dp', 'blk'), may hold values from -6 to 6
- model_side_factors: bfloat16 [2, 32, 16384], P(None, 'dp', 'blk'), may hold values from -0.046875 to 0.046875
- hidden_side_factors: bfloat16 [2, 32, 53248], P(None, 'dp', 'blk'), may hold values from -0.02734375 to 0.02734375
- example_index_rows: int32 [32, 288], P('dp'), may hold values from 0 to 7, never falling along the last dimension, each value on 1 to 72 neighbouring positions
- clipping_threshold: int32 [1], replicated, may hold values from 0 to 7
- model_side_noise: float32 [2, 32, 16384], P(None, 'dp', 'blk'), may hold values from -6 to 6
- hidden_side_noise: float32 [2, 32, 53248], P(None, 'dp', 'blk'), may hold values from -6 to 6
Outputs:
- update_model: float32 [2, 32, 16384], P(None, 'dp', 'blk')
- update_hidden: float32 [2, 32, 53248], P(None, 'dp', 'blk')
Inputs may be any that keep to these rules, and one draw needn't show every extreme that they name: `example_index_rows`: along each row the ids never fall, every id 0 to 7 occurs, and an example has at most 72 tokens, some example exactly that many.
All inputs are finite; a program needn't handle non-finite values.
Results may differ from a plain program's by a relative error of at most 0.0003.
Values may be sent and summed in bfloat16 or wider, within the bound.
A program may use at most 64 MiB of HBM per device.

v0:
```python
import jax
import jax.numpy as jnp
from jax import lax
from jax.sharding import PartitionSpec as P

EX = 8


def copy_for_each(shard, axis):
    copies = jnp.broadcast_to(shard, (lax.axis_size(axis), *shard.shape))
    return lax.all_to_all(copies, axis, split_axis=0, concat_axis=0, tiled=True)


def over_copies(shard, axis):
    everything = copy_for_each(shard, axis)
    return jnp.sum(everything, axis=0)


def sent_together(arrays, axis, dim, along):
    widths = [a.shape[along] for a in arrays]
    both = jnp.concatenate(arrays, axis=along)
    whole = lax.all_gather(both, axis, axis=dim, tiled=True)
    return tuple(jnp.split(whole, [sum(widths[:k]) for k in range(1, len(widths))], axis=along))


def in_blocks(shard, dim, devices):
    before, after = (shard.shape[:dim], shard.shape[dim + 1 :])
    return jnp.moveaxis(shard.reshape(*before, devices, -1, *after), dim, 0)


def sum_at_owner(shard, axis, dim):
    devices = lax.axis_size(axis)
    blocks = lax.all_to_all(in_blocks(shard, dim, devices), axis, 0, 0, tiled=True)
    return jnp.sum(blocks, axis=0)


def rows_for(lines, devices):
    spare = -lines.shape[0] % devices
    if not spare:
        return lines
    return jnp.concatenate([lines, jnp.zeros((spare, *lines.shape[1:]), lines.dtype)])


def joined_along(blocks, dim):
    shape = list(blocks.shape[1:])
    shape[dim] *= blocks.shape[0]
    return jnp.moveaxis(blocks, 0, dim).reshape(shape)


def gather_directly(shard, axis, dim):
    blocks = copy_for_each(shard, axis)
    return joined_along(blocks, dim)


def sum_by_parts(shard, axes):
    lines = shard.reshape(-1, shard.shape[-1])
    own = sum_at_owner(rows_for(lines, lax.axis_size(axes)), axes, 0)
    whole = gather_directly(own, axes, 0)
    return whole[: len(lines)].reshape(shard.shape)


def side_by_side(arrays, axis, dim, along):
    widths = [a.shape[along] for a in arrays]
    both = jnp.concatenate(arrays, axis=along)
    whole = sum_at_owner(both, axis, dim)
    return tuple(jnp.split(whole, [sum(widths[:k]) for k in range(1, len(widths))], axis=along))


def total_over_groups(local_sum):
    return over_copies(local_sum, "dp")


def example_grads(member, narrow, broad):
    weighted = member[:, :, None] * narrow[None, :, :]
    return jnp.einsum(
        "etr,tf->erf",
        weighted,
        broad,
        precision=lax.Precision.HIGHEST,
        preferred_element_type=jnp.float32,
    )


def per_device(
    block_input_rows,
    up_loss_gradient,
    down_projection_input,
    output_loss_gradient,
    model_side_factors,
    hidden_side_factors,
    example_index_rows,
    clipping_threshold,
    model_side_noise,
    hidden_side_noise,
):
    model_full, hidden_full = sent_together((model_side_factors, hidden_side_factors), "dp", 1, 2)
    input_projected = jnp.dot(block_input_rows, model_full[0].T, preferred_element_type=jnp.float32)
    up_backward = jnp.dot(up_loss_gradient, hidden_full[0].T, preferred_element_type=jnp.float32)
    hidden_projected = jnp.dot(
        down_projection_input, hidden_full[1].T, preferred_element_type=jnp.float32
    )
    down_backward = jnp.dot(
        output_loss_gradient, model_full[1].T, preferred_element_type=jnp.float32
    )
    partial_value = jnp.stack([input_projected, up_backward, hidden_projected, down_backward])
    doc_ids = example_index_rows[0]
    num_examples = EX
    member = (doc_ids[None, :] == jnp.arange(num_examples, dtype=jnp.int32)[:, None]).astype(
        jnp.float32
    )
    groups = lax.axis_size("dp")
    projected = sum_by_parts(partial_value, "blk")
    per_model = jnp.stack(
        [
            example_grads(member, projected[1], block_input_rows),
            example_grads(member, projected[2], output_loss_gradient),
        ]
    )
    per_hidden = jnp.stack(
        [
            example_grads(member, projected[0], up_loss_gradient),
            example_grads(member, projected[3], down_projection_input),
        ]
    )
    part_sq = jnp.sum(per_model * per_model, axis=(0, 2, 3)) + jnp.sum(
        per_hidden * per_hidden, axis=(0, 2, 3)
    )
    norm_sq = over_copies(part_sq, "blk")
    grand_total = total_over_groups(jnp.sum(norm_sq))
    root_mean = jnp.sqrt(grand_total / (groups * num_examples) + 1e-06)
    clip_bound = (0.5 + 0.125 * clipping_threshold[0].astype(jnp.float32)) * root_mean
    factors = jnp.minimum(1.0, clip_bound * lax.rsqrt(norm_sq + 1e-06))
    grad_model = jnp.einsum("e,kerf->krf", factors, per_model, precision=lax.Precision.HIGHEST)
    grad_hidden = jnp.einsum("e,kerf->krf", factors, per_hidden, precision=lax.Precision.HIGHEST)
    summed_model, summed_hidden = side_by_side((grad_model, grad_hidden), "dp", 1, 2)
    blocks = lax.axis_size("blk")
    rank = model_full.shape[1]
    width = block_input_rows.shape[1] * blocks
    hidden_width = down_projection_input.shape[1] * blocks
    rescale = (
        jnp.sqrt(jnp.float32(2 * rank * (width + hidden_width)) / (groups * num_examples))
        / clip_bound
    )
    return (summed_model * rescale + model_side_noise, summed_hidden * rescale + hidden_side_noise)


def solution(mesh):
    in_specs = (
        P("dp", "blk"),
        P("dp", "blk"),
        P("dp", "blk"),
        P("dp", "blk"),
        P(None, "dp", "blk"),
        P(None, "dp", "blk"),
        P("dp", None),
        P(),
        P(None, "dp", "blk"),
        P(None, "dp", "blk"),
    )
    out_specs = (P(None, "dp", "blk"), P(None, "dp", "blk"))
    return jax.shard_map(
        per_device, mesh=mesh, in_specs=in_specs, out_specs=out_specs, check_vma=False
    )
```

profile of v0, /device:TPU:1, one launch (start us, length us, event | category | flops | bytes accessed | tf_op | source)
XLA Modules:
  0.0 219.3 jit_solution(5735597681922689912)
XLA Ops:
  0.6 0.9 pad_maximum_fusion.3
  1.5 47.5 %all_gather.3 = bf16[2,32,4352]{2,0,1:T(2,128)(2,1)S(1)} all-gather(bf16[2,1,4352]{2,0,1:T(2,128)(2,1)S(1)} %pad_maximum_fusion.3), channel_id=1, replica_groups=mesh['dp'=32,'blk'=16] {'dp'}, dimensions={1}, use_global_device_ids=true | all-gather | bytes 574464 | tf_op jit(solution)/shard_map/all_gather | solution.py:22
  49.0 0.6 fusion.27
  49.8 0.6 convolution_bitcast_fusion.5
  50.5 0.7 convolution_bitcast_fusion.6
  52.2 31.5 %all_to_all.27 = f32[16,72,32]{1,2,0:T(8,128)S(1)} all-to-all(f32[16,72,32]{1,2,0:T(8,128)S(1)} %copy.46), channel_id=1, replica_groups=mesh['dp'=32,'blk'=16] {'blk'}, dimensions={0} | all-to-all | bytes 294912 | tf_op jit(solution)/shard_map/all_to_all | solution.py:33
  83.7 0.7 broadcast_in_dim.6
  84.4 4.7 %all-to-all-start.1 = ((f32[16,72,32]{1,2,0:T(8,128)}), f32[16,72,32]{1,2,0:T(8,128)S(1)}, u32[]{:S(2)}, u32[]{:S(2)}) async-start(f32[16,72,32]{1,2,0:T(8,128)} %broadcast_in_dim.6), calls=%async_computation.1 | async-start | bytes 524288 | tf_op jit(solution)/shard_map/all_to_all | solution.py:11
  89.2 16.1 %all-to-all-done.1 = f32[16,72,32]{1,2,0:T(8,128)S(1)} async-done(((f32[16,72,32]{1,2,0:T(8,128)}), f32[16,72,32]{1,2,0:T(8,128)S(1)}, u32[]{:S(2)}, u32[]{:S(2)}) %all-to-all-start.1) | async-done | bytes 147488 | tf_op jit(solution)/shard_map/all_to_all | solution.py:11
  105.3 0.6 fusion.28
  106.3 4.6 %convolution_bitcast_fusion = f32[1,8,32,3328]{3,2,1,0:T(8,128)} fusion(bf16[288,3328]{1,0:T(8,128)(2,1)S(1)} %copy-done, f32[288,32]{0,1:T(8,128)S(1)} %mul.92, f32[8,288]{1,0:T(8,128)S(1)} %fusion.21), kind=kOutput, calls=%fused_computation.4 | convolution fusion | flops 2944475136 | bytes 5370880 | tf_op jit(solution)/shard_map/etr,tf->erf/dot_general | solution.py:75
  110.9 4.7 %convolution_bitcast_fusion.1 = f32[1,8,32,3328]{3,2,1,0:T(8,128)} fusion(bf16[288,3328]{1,0:T(8,128)(2,1)S(1)} %copy-done.2, f32[288,32]{0,1:T(8,128)S(1)} %mul.89, f32[8,288]{1,0:T(8,128)S(1)} %fusion.21), kind=kOutput, calls=%fused_computation.5 | convolution fusion | flops 2944475136 | bytes 5370880 | tf_op jit(solution)/shard_map/etr,tf->erf/dot_general | solution.py:75
  115.6 0.7 mul.85
  116.3 1.8 convolution_bitcast_fusion.2
  118.1 0.9 copy.47
  119.1 2.1 convolution_bitcast_fusion.3
  121.2 6.5 %multiply_reduce_fusion = (f32[8]{0:T(128)S(1)}, f32[2,8,32,3328]{3,2,1,0:T(8,128)}) fusion(f32[1,8,32,3328]{3,2,1,0:T(8,128)} %convolution_bitcast_fusion, f32[1,8,32,3328]{3,2,1,0:T(8,128)} %convolution_bitcast_fusion.1), kind=kLoop, calls=%fused_computation.3 | loop fusion | flops 5111800 | bytes 13631520 | tf_op jit(solution)/shard_map/reduce_sum | solution.py:125
  127.7 1.6 pad_maximum_fusion.1
  129.4 19.6 %all_to_all.28 = f32[16,1,8]{2,1,0:T(1,128)S(1)} all-to-all(f32[16,1,8]{2,1,0:T(1,128)S(1)} %broadcast_in_dim.7), channel_id=1, replica_groups=mesh['dp'=32,'blk'=16] {'blk'}, dimensions={0} | all-to-all | bytes 1024 | tf_op jit(solution)/shard_map/all_to_all | solution.py:11
  149.0 0.6 fusion.25
  149.6 1.3 broadcast_in_dim.16
  150.8 6.7 %all-to-all-start.3 = ((f32[32,1,1]{2,1,0:T(1,128)}), f32[32,1,1]{2,1,0:T(1,128)S(1)}, u32[]{:S(2)}, u32[]{:S(2)}) async-start(f32[32,1,1]{2,1,0:T(1,128)} %broadcast_in_dim.16), calls=%async_computation.3 | async-start | bytes 32768 | tf_op jit(solution)/shard_map/all_to_all | solution.py:11
  158.2 6.7 %all-to-all-done.3 = f32[32,1,1]{2,1,0:T(1,128)S(1)} async-done(((f32[32,1,1]{2,1,0:T(1,128)}), f32[32,1,1]{2,1,0:T(1,128)S(1)}, u32[]{:S(2)}, u32[]{:S(2)}) %all-to-all-start.3) | async-done | bytes 160 | tf_op jit(solution)/shard_map/all_to_all | solution.py:11
  164.9 0.6 reduce_sum.69
  166.2 4.4 %fusion.2 = f32[1,2,32,1024]{3,0,2,1:T(1,128)S(1)} fusion(f32[2,8,32,1024]{3,2,1,0:T(8,128)} %get-tuple-element.6, f32[8]{0:T(128)S(1)} %get-tuple-element.3, f32[]{:T(128)S(6)} %mul.96), kind=kOutput, calls=%fused_computation.7 | convolution fusion | flops 6291480 | bytes 2359332 | tf_op jit(solution)/shard_map/e,kerf->krf/dot_general | solution.py:133
  170.9 12.3 %fusion = f32[1,2,32,3328]{3,0,2,1:T(1,128)S(1)} fusion(f32[2,8,32,3328]{3,2,1,0:T(8,128)} %get-tuple-element.5, f32[8]{0:T(128)S(1)} %get-tuple-element.3, f32[]{:T(128)S(6)} %mul.96), kind=kOutput, calls=%fused_computation.1 | convolution fusion | flops 20447256 | bytes 7667748 | tf_op jit(solution)/shard_map/e,kerf->krf/dot_general | solution.py:134
  183.2 0.7 copy.81
  183.8 1.5 maximum_bitcast_fusion
  185.3 4.4 %all-to-all-start.4 = ((f32[32,2,1,4352]{3,1,2,0:T(2,128)}), f32[32,2,1,4352]{3,1,2,0:T(2,128)S(1)}, u32[]{:S(2)}, u32[]{:S(2)}) async-start(f32[32,2,1,4352]{3,1,2,0:T(2,128)} %maximum_bitcast_fusion), calls=%async_computation.4 | async-start | bytes 2228224 | tf_op jit(solution)/shard_map/all_to_all | solution.py:33
  189.7 28.0 %all-to-all-done.4 = f32[32,2,1,4352]{3,1,2,0:T(2,128)S(1)} async-done(((f32[32,2,1,4352]{3,1,2,0:T(2,128)}), f32[32,2,1,4352]{3,1,2,0:T(2,128)S(1)}, u32[]{:S(2)}, u32[]{:S(2)}) %all-to-all-start.4) | async-done | bytes 1114144 | tf_op jit(solution)/shard_map/all_to_all | solution.py:33
  218.1 0.6 fusion.20
  218.7 0.6 fusion.22
  (39 shorter events, 2.3 us)
Async XLA Ops:
  0.6 49.1 %copy-start = (bf16[288,3328]{1,0:T(8,128)(2,1)S(1)}, bf16[288,3328]{1,0:T(8,128)(2,1)}, u32[]{:S(2)}) copy-start(bf16[288,3328]{1,0:T(8,128)(2,1)} %param.12) | copy-start | bytes 5750788
  49.0 1.5 copy-start.1
  49.8 1.4 copy-start.3
  49.8 1.7 copy-start.4
  51.5 37.7 %copy-start.8 = (s32[1,288]{1,0:T(1,128)S(1)}, s32[1,288]{1,0:T(1,128)}, u32[]{:S(2)}) copy-start(s32[1,288]{1,0:T(1,128)} %param.16) | copy-start | bytes 3460
  84.4 20.9 %all-to-all-start.1 = ((f32[16,72,32]{1,2,0:T(8,128)}), f32[16,72,32]{1,2,0:T(8,128)S(1)}, u32[]{:S(2)}, u32[]{:S(2)}) async-start(f32[16,72,32]{1,2,0:T(8,128)} %broadcast_in_dim.6), calls=%async_computation.1 | async-start | bytes 524288 | tf_op jit(solution)/shard_map/all_to_all | solution.py:11
  89.2 21.7 %copy-start.5 = (f32[8,288]{1,0:T(8,128)}, f32[8,288]{1,0:T(8,128)S(1)}, u32[]{:S(2)}) copy-start(f32[8,288]{1,0:T(8,128)S(1)} %fusion.21) | copy-start | bytes 27652
  106.3 4.6 %copy-start.2 = (bf16[288,3328]{1,0:T(8,128)(2,1)S(1)}, bf16[288,3328]{1,0:T(8,128)(2,1)}, u32[]{:S(2)}) copy-start(bf16[288,3328]{1,0:T(8,128)(2,1)} %param.11) | copy-start | bytes 5750788
  150.8 14.1 %all-to-all-start.3 = ((f32[32,1,1]{2,1,0:T(1,128)}), f32[32,1,1]{2,1,0:T(1,128)S(1)}, u32[]{:S(2)}, u32[]{:S(2)}) async-start(f32[32,1,1]{2,1,0:T(1,128)} %broadcast_in_dim.16), calls=%async_computation.3 | async-start | bytes 32768 | tf_op jit(solution)/shard_map/all_to_all | solution.py:11
  185.3 32.8 %copy-start.6 = (f32[2,1,3328]{2,1,0:T(1,128)S(1)}, f32[2,1,3328]{2,1,0:T(1,128)}, u32[]{:S(2)}) copy-start(f32[2,1,3328]{2,1,0:T(1,128)} %param.19) | copy-start | bytes 79876
  185.3 33.4 %copy-start.7 = (f32[2,1,1024]{2,1,0:T(1,128)S(1)}, f32[2,1,1024]{2,1,0:T(1,128)}, u32[]{:S(2)}) copy-start(f32[2,1,1024]{2,1,0:T(1,128)} %param.18) | copy-start | bytes 24580
  185.3 32.4 %all-to-all-start.4 = ((f32[32,2,1,4352]{3,1,2,0:T(2,128)}), f32[32,2,1,4352]{3,1,2,0:T(2,128)S(1)}, u32[]{:S(2)}, u32[]{:S(2)}) async-start(f32[32,2,1,4352]{3,1,2,0:T(2,128)} %maximum_bitcast_fusion), calls=%async_computation.4 | async-start | bytes 2228224 | tf_op jit(solution)/shard_map/all_to_all | solution.py:33
where the time goes:
time: 220 us; the launch traced here: 219 us
  blocking collectives  98.5 us (45%)
  waiting for transfers between devices  50.9 us (23%)
  matrix products  31.7 us (14%)
  starting transfers between devices  15.8 us (7%)
  other arithmetic  13.4 us (6%)
  local copies, waits for them, and re-layouts  6.77 us (3%)
  between operations  2.3 us (1%)
    all_gather x1, blocking collectives, sent_together(): whole = lax.all_gather(both, axis, axis=dim, tiled=True)  47.5 us
    all_to_all x1, blocking collectives, sum_at_owner(): lax.all_to_all(in_blocks(shard, dim, devices), axis, 0, 0, tiled=True)  31.5 us
    all_to_all x1, waiting for transfers between devices, sum_at_owner(): lax.all_to_all(in_blocks(shard, dim, devices), axis, 0, 0, tiled=True)  28 us
    all_to_all x2, waiting for transfers between devices, copy_for_each(): return lax.all_to_all(copies, axis, split_axis=0, concat_axis=0, tiled=True)  22.9 us
    all_to_all x1, blocking collectives, copy_for_each(): return lax.all_to_all(copies, axis, split_axis=0, concat_axis=0, tiled=True)  19.6 us
    dot_general x4, matrix products, example_grads(): jnp.einsum('etr,tf->erf', weighted, broad, precision=lax.Precision.HIGHES...  13.1 us
    dot_general x1, matrix products, per_device(): jnp.einsum('e,kerf->krf', factors, per_hidden, precision=lax.Precision.HI...  12.3 us
    all_to_all x2, starting transfers between devices, copy_for_each(): return lax.all_to_all(copies, axis, split_axis=0, concat_axis=0, tiled=True)  11.4 us
  transfers between devices with their start and end apart: 3, of which 3 were waited for; matrix products, arithmetic and copies ran while one was open for 0% of the time, Pallas kernels for 0%

commit v1 on v0

v1 whole, which is shorter than its diff:
```python
import functools
import math

import jax
import jax.numpy as jnp
from jax import lax
from jax.experimental import pallas as pl
from jax.experimental.pallas import tpu as pltpu
from jax.sharding import PartitionSpec as P

EX = 8
LANES = 128
SLOT = 32
DP_AXES = {32: (4, 4, 2), 4: (2, 1, 2), 8: (2, 2, 2)}
BLK_AXES = {16: (4, 4), 4: (2, 2), 2: (1, 2)}
PAIR = (1, 0, 3, 2)
F32 = jnp.float32
BF16 = jnp.bfloat16


def nt(a, b):
    return lax.dot_general(a, b, (((1,), (1,)), ((), ())), preferred_element_type=F32)


def nn(a, b):
    return lax.dot_general(a, b, (((1,), (0,)), ((), ())), preferred_element_type=F32)


def split(a):
    high = a.astype(BF16)
    return high, (a - high.astype(F32)).astype(BF16)


def remote(src, dst, send, recv, **where):
    return pltpu.make_async_remote_copy(
        src_ref=src,
        dst_ref=dst,
        send_sem=send,
        recv_sem=recv,
        device_id=where,
        device_id_type=pl.DeviceIdType.MESH,
    )


def kernel(
    cfg,
    thr_ref,
    ids_ref,
    row_ref,
    a0,
    a1,
    a2,
    a3,
    out_ref,
    wide,
    rows_in,
    rows_f32,
    factors,
    gram_hi,
    gram_lo,
    part,
    part_in,
    quarter,
    quarter_in,
    proj,
    plane,
    ring,
    grads,
    pair_in,
    pair_sum,
    y_in,
    z_out,
    z_in,
    load_sem,
    row_send,
    row_recv,
    part_send,
    part_recv,
    quarter_send,
    quarter_recv,
    proj_send,
    proj_recv,
    plane_send,
    plane_recv,
    ring_send,
    ring_recv,
    pair_send,
    pair_recv,
    y_send,
    y_recv,
    z_send,
    z_recv,
):
    NZL, NY, NC, NX, NZH, widths, block = cfg
    tokens = wide.shape[0]
    ranks = NZL * NY * NC
    dp, blk = lax.axis_index("dp"), lax.axis_index("blk")
    zl, y, c = dp // (NY * NC), (dp // NC) % NY, dp % NC
    x, zh = blk // NZH, blk % NZH
    nz, npl = NZL * NZH, NX * NY * NC
    zz = zh * NZL + zl
    pp = (x * NY + y) * NC + c

    def dp_of(z_, y_, c_):
        return (z_ * NY + y_) * NC + c_

    def slot_of(z_, y_, c_):
        return (c_ * NZL + z_) * NY + y_

    def plane_where(k):
        q = (pp + k) % npl
        x_, y_, c_ = q // (NY * NC), (q // NC) % NY, q % NC
        return {"dp": dp_of(zl, y_, c_), "blk": x_ * NZH + zh}

    def ring_where(k):
        q = (zz + k) % nz
        return {"dp": dp_of(q % NZL, y, c), "blk": x * NZH + q // NZL}

    offsets = [sum(widths[:i]) for i in range(4)]
    loads = []
    for i, ref in enumerate((a0, a1, a2, a3)):
        copy = pltpu.make_async_copy(
            ref, wide.at[:, pl.ds(offsets[i], widths[i])], load_sem.at[i]
        )
        copy.start()
        loads.append(copy)

    barrier = pltpu.get_barrier_semaphore()

    def greet_plane(k, carry):
        pl.semaphore_signal(
            barrier, inc=1, device_id=plane_where(k), device_id_type=pl.DeviceIdType.MESH
        )
        return carry

    def greet_ring(k, carry):
        pl.semaphore_signal(
            barrier, inc=1, device_id=ring_where(k), device_id_type=pl.DeviceIdType.MESH
        )
        return carry

    lax.fori_loop(1, npl, greet_plane, 0)
    lax.fori_loop(1, nz, greet_ring, 0)

    half, reach = tokens // 2, 256
    member_t = (
        jnp.broadcast_to(ids_ref[...], (LANES, tokens))
        == lax.broadcasted_iota(jnp.int32, (LANES, tokens), 0)
    ).astype(F32).astype(BF16)
    eye = (
        lax.broadcasted_iota(jnp.int32, (tokens, tokens), 0)
        == lax.broadcasted_iota(jnp.int32, (tokens, tokens), 1)
    ).astype(F32).astype(BF16)
    member = nt(eye, member_t)
    member_b = member.astype(BF16)
    starts = (0, tokens - reach)
    factors[...] = jnp.zeros_like(factors)

    pl.semaphore_wait(barrier, npl - 1 + nz - 1)

    own = slot_of(zl, y, c)
    sends = []

    def row_copy(src, slot, where):
        copy = remote(src, rows_in.at[slot], row_send.at[len(sends)], row_recv.at[slot], dp=where)
        copy.start()
        sends.append(copy)

    def row_wait(slot):
        remote(
            rows_in.at[slot], rows_in.at[slot], row_send.at[0], row_recv.at[slot], dp=dp_of(zl, y, 1 - c)
        ).wait_recv()

    for k in range(1, NZL):
        row_copy(row_ref, own, dp_of((zl + k) % NZL, y, c))
    for j in range(1, NY):
        row_copy(row_ref, own, dp_of(zl, (y + j) % NY, c))
    row_copy(row_ref, own, dp_of(zl, y, 1 - c))

    for i in (0, 3, 1, 2):
        loads[i].wait()
        for b in range(2):
            same = nt(member_b[b * half : (b + 1) * half], member_b[starts[b] : starts[b] + reach])
            total = jnp.zeros((half, reach), F32)
            for k in range(0, widths[i], 256):
                n = min(256, widths[i] - k)
                at = offsets[i] + k
                total += nt(
                    wide[b * half : (b + 1) * half, at : at + n],
                    wide[starts[b] : starts[b] + reach, at : at + n],
                )
            high, low = split(jnp.where(same > 0.5, total, 0.0))
            gram_hi[i, b] = high
            gram_lo[i, b] = low

    for k in range(1, NZL):
        z_ = (zl + k) % NZL
        slot = slot_of(z_, y, c)
        row_wait(slot)
        for j in range(1, NY):
            row_copy(rows_in.at[slot], slot, dp_of(zl, (y + j) % NY, c))
        row_copy(rows_in.at[slot], slot, dp_of(zl, y, 1 - c))
    for k in range(NZL):
        for j in range(1, NY):
            slot = slot_of((zl + k) % NZL, (y + j) % NY, c)
            row_wait(slot)
            row_copy(rows_in.at[slot], slot, dp_of(zl, y, 1 - c))

    def widen(ref, slot):
        at = pl.multiple_of(slot * block, 8)
        rows_f32[pl.ds(at, block), :] = ref[...].astype(F32)[:block]

    widen(row_ref, own)
    for k in range(NZL):
        for j in range(NY):
            if k or j:
                slot = slot_of((zl + k) % NZL, (y + j) % NY, c)
                widen(rows_in.at[slot], slot)
    for k in range(NZL):
        for j in range(NY):
            slot = slot_of((zl + k) % NZL, (y + j) % NY, 1 - c)
            row_wait(slot)
            widen(rows_in.at[slot], slot)

    chunks = [w // LANES for w in widths]
    firsts = (0, chunks[0] + chunks[3], chunks[0] + chunks[3] + chunks[1], chunks[0])
    for i in range(4):
        for j in range(chunks[i]):
            picked = rows_f32[pl.ds(firsts[i] + j, ranks, stride=block), :]
            at = offsets[i] + j * LANES
            factors[SLOT * i : SLOT * i + ranks, at : at + LANES] = picked.astype(BF16)

    total = jnp.zeros((tokens, LANES), F32)
    for k in range(0, wide.shape[1], 256):
        n = min(256, wide.shape[1] - k)
        total += nt(wide[:, k : k + n], factors[:, k : k + n])
    part[...] = total.reshape(part.shape)

    copies = []
    for k in range(1, NX):
        x_ = (x + k) % NX
        copy = remote(
            part.at[x_], part_in.at[x], part_send.at[k], part_recv.at[k], blk=x_ * NZH + zh
        )
        copy.start()
        copies.append(copy)
    for copy in copies:
        copy.wait_recv()
    held = part[x]
    for k in range(1, NX):
        held += part_in[(x + k) % NX]
    quarter[...] = held
    sends += copies
    copies = []
    for k in range(1, NZH):
        copy = remote(
            quarter,
            quarter_in.at[zh],
            quarter_send.at[k],
            quarter_recv.at[k],
            blk=x * NZH + (zh + k) % NZH,
        )
        copy.start()
        copies.append(copy)
    for copy in copies:
        copy.wait_recv()
    for k in range(1, NZH):
        held += quarter_in[(zh + k) % NZH]
    proj[x] = held
    sends += copies
    copies = []
    for k in range(1, NX):
        copy = remote(
            proj.at[x], proj.at[x], proj_send.at[k], proj_recv.at[k], blk=((x + k) % NX) * NZH + zh
        )
        copy.start()
        copies.append(copy)
    for copy in copies:
        copy.wait_recv()
    sends += copies

    sums = proj[...].reshape(tokens, LANES)
    high, low = split(sums)
    both = jnp.concatenate([high, low], axis=1)
    lane = lax.broadcasted_iota(jnp.int32, (half, LANES), 1) // SLOT
    norm = jnp.zeros((1, LANES), F32)
    for b in range(2):
        mixed = jnp.zeros((half, LANES), F32)
        for i in range(4):
            first = nn(gram_hi[i, b], both[starts[b] : starts[b] + reach])
            second = nn(gram_lo[i, b], high[starts[b] : starts[b] + reach])
            term = first[:, :LANES] + first[:, LANES:] + second
            mixed = jnp.where(lane == PAIR[i], term, mixed)
        mine = sums[b * half : (b + 1) * half]
        each = jnp.sum(mixed * mine, axis=1, keepdims=True)
        norm += jnp.sum(member[b * half : (b + 1) * half] * each, axis=0, keepdims=True)

    plane[pp] = norm

    def plane_copy(k):
        return remote(plane.at[pp], plane.at[pp], plane_send, plane_recv, **plane_where(k))

    def plane_start(k, carry):
        plane_copy(k).start()
        return carry

    lax.fori_loop(1, npl, plane_start, 0)
    rest = plane.at[pl.ds(0, npl - 1)]
    remote(rest, rest, plane_send, plane_recv, **plane_where(1)).wait()
    everyone = jnp.sum(plane[...], axis=0)
    group = jnp.zeros((1, LANES), F32)
    for k in range(NX):
        group += plane[(k * NY + y) * NC + c]
    ring[zz] = jnp.concatenate([group, everyone], axis=0)

    def ring_start(k, carry):
        remote(ring.at[zz], ring.at[zz], ring_send, ring_recv, **ring_where(k)).start()
        return carry

    lax.fori_loop(1, nz, ring_start, 0)
    rest = ring.at[pl.ds(0, nz - 1)]
    remote(rest, rest, ring_send, ring_recv, **ring_where(1)).wait()
    everyone = jnp.sum(ring[...], axis=0)[1:2]
    group = jnp.zeros((1, LANES), F32)
    for k in range(NZH):
        group += ring[k * NZL + zl][0:1]
    grand_total = jnp.sum(everyone, axis=1, keepdims=True)
    root_mean = jnp.sqrt(jnp.maximum(grand_total, 0.0) / (ranks * EX) + 1e-06)
    clip = (0.5 + 0.125 * thr_ref[0].astype(F32)) * root_mean
    factor = jnp.minimum(1.0, clip * lax.rsqrt(jnp.maximum(group, 0.0) + 1e-06))
    entries = 2 * ranks * NX * NZH * (widths[0] + widths[1])
    rescale = math.sqrt(entries / (ranks * EX)) / clip
    weight = jnp.sum(member * (factor * rescale), axis=1, keepdims=True)

    high, low = split(weight * sums)
    eye = (
        lax.broadcasted_iota(jnp.int32, (LANES, LANES), 0)
        == lax.broadcasted_iota(jnp.int32, (LANES, LANES), 1)
    ).astype(F32).astype(BF16)
    high_t, low_t = nt(eye, high).astype(BF16), nt(eye, low).astype(BF16)
    for i in range(4):
        at = SLOT * PAIR[i]
        left = jnp.concatenate([high_t[at : at + SLOT], low_t[at : at + SLOT]], axis=0)
        for k in range(0, widths[i], 256):
            n = min(256, widths[i] - k)
            got = nn(left, wide[:, offsets[i] + k : offsets[i] + k + n])
            got = got[:SLOT] + got[SLOT:]
            for j in range(n // LANES):
                grads[pl.ds(firsts[i] + k // LANES + j, ranks, stride=block), :] = got[
                    :ranks, j * LANES : (j + 1) * LANES
                ]

    wide_block = NY * block
    copies = []
    for k in list(range(1, NZL)) + [0]:
        z_ = (zl + k) % NZL
        at = pl.multiple_of(((1 - c) * NZL + z_) * wide_block, 8)
        copy = remote(
            grads.at[pl.ds(at, wide_block)],
            pair_in.at[z_],
            pair_send.at[k],
            pair_recv.at[k],
            dp=dp_of(zl, y, 1 - c),
        )
        copy.start()
        copies.append(copy)
    sends += copies
    y_copies = {}
    for copy, k in zip(copies, list(range(1, NZL)) + [0]):
        z_ = (zl + k) % NZL
        at = pl.multiple_of((c * NZL + z_) * wide_block, 8)
        copy.wait_recv()
        pair_sum[z_] = (grads[pl.ds(at, wide_block), :] + pair_in[z_]).reshape(NY, block, LANES)
        for j in range(1, NY):
            y_ = (y + j) % NY
            copy = remote(
                pair_sum.at[z_, y_],
                y_in.at[z_, y],
                y_send.at[k, j],
                y_recv.at[k, j],
                dp=dp_of(zl, y_, c),
            )
            copy.start()
            y_copies[k, j] = copy
    z_copies = []
    for k in list(range(1, NZL)) + [0]:
        z_ = (zl + k) % NZL
        held = pair_sum[z_, y]
        for j in range(1, NY):
            y_copies[k, j].wait_recv()
            sends.append(y_copies[k, j])
        for j in range(1, NY):
            held += y_in[z_, (y + j) % NY]
        if k:
            z_out[k] = held
            copy = remote(
                z_out.at[k], z_in.at[zl], z_send.at[k], z_recv.at[k], dp=dp_of(z_, y, c)
            )
            copy.start()
            z_copies.append(copy)
    for copy in z_copies:
        copy.wait_recv()
    for k in range(1, NZL):
        held += z_in[(zl + k) % NZL]
    out_ref[...] = held
    for copy in sends + z_copies:
        copy.wait_send()


def per_device(
    nx,
    block_input_rows,
    up_loss_gradient,
    down_projection_input,
    output_loss_gradient,
    model_side_factors,
    hidden_side_factors,
    example_index_rows,
    clipping_threshold,
    model_side_noise,
    hidden_side_noise,
):
    ndp, nblk = lax.axis_size("dp"), lax.axis_size("blk")
    NZL, NY, NC = DP_AXES[ndp]
    NX, NZH = BLK_AXES[nblk]
    tokens = block_input_rows.shape[0]
    model, hidden = block_input_rows.shape[1], up_loss_gradient.shape[1]
    widths = (model, hidden, hidden, model)
    total = sum(widths)
    rows = total // LANES
    block = -(-rows // 8) * 8
    sent = -(-rows // 16) * 16
    own = jnp.concatenate(
        [
            model_side_factors.reshape(-1, LANES),
            hidden_side_factors.reshape(-1, LANES),
            jnp.zeros((sent - rows, LANES), BF16),
        ]
    )
    cfg = (NZL, NY, NC, NX, NZH, widths, block)
    half, reach = tokens // 2, 256
    dma = pltpu.SemaphoreType.DMA
    vmem = pl.BlockSpec(memory_space=pltpu.VMEM)
    hbm = pl.BlockSpec(memory_space=pl.ANY)
    summed = pl.pallas_call(
        functools.partial(kernel, cfg),
        out_shape=jax.ShapeDtypeStruct((block, LANES), F32),
        in_specs=[pl.BlockSpec(memory_space=pltpu.SMEM), vmem, vmem, hbm, hbm, hbm, hbm],
        out_specs=vmem,
        scratch_shapes=[
            pltpu.VMEM((tokens, total), BF16),
            pltpu.VMEM((ndp, sent, LANES), BF16),
            pltpu.VMEM((ndp * block, LANES), F32),
            pltpu.VMEM((LANES, total), BF16),
            pltpu.VMEM((4, 2, half, reach), BF16),
            pltpu.VMEM((4, 2, half, reach), BF16),
            pltpu.VMEM((NX, tokens // NX, LANES), F32),
            pltpu.VMEM((NX, tokens // NX, LANES), F32),
            pltpu.VMEM((tokens // NX, LANES), F32),
            pltpu.VMEM((NZH, tokens // NX, LANES), F32),
            pltpu.VMEM((NX, tokens // NX, LANES), F32),
            pltpu.VMEM((NX * NY * NC, 1, LANES), F32),
            pltpu.VMEM((NZL * NZH, 2, LANES), F32),
            pltpu.VMEM((ndp * block, LANES), F32),
            pltpu.VMEM((NZL, NY * block, LANES), F32),
            pltpu.VMEM((NZL, NY, block, LANES), F32),
            pltpu.VMEM((NZL, NY, block, LANES), F32),
            pltpu.VMEM((NZL, block, LANES), F32),
            pltpu.VMEM((NZL, block, LANES), F32),
            dma((4,)),
            dma((ndp,)),
            dma((ndp,)),
            dma((NX,)),
            dma((NX,)),
            dma((NZH,)),
            dma((NZH,)),
            dma((NX,)),
            dma((NX,)),
            dma,
            dma,
            dma,
            dma,
            dma((NZL,)),
            dma((NZL,)),
            dma((NZL, NY)),
            dma((NZL, NY)),
            dma((NZL,)),
            dma((NZL,)),
        ],
        compiler_params=pltpu.CompilerParams(
            collective_id=0, has_side_effects=True, vmem_limit_bytes=56 << 20
        ),
        name="clipped_step",
    )(
        clipping_threshold,
        example_index_rows,
        own,
        block_input_rows,
        up_loss_gradient,
        down_projection_input,
        output_loss_gradient,
    )
    cut = 2 * model // LANES
    return (
        summed[:cut].reshape(model_side_noise.shape) + model_side_noise,
        summed[cut:rows].reshape(hidden_side_noise.shape) + hidden_side_noise,
    )


def solution(mesh):
    in_specs = (
        P("dp", "blk"),
        P("dp", "blk"),
        P("dp", "blk"),
        P("dp", "blk"),
        P(None, "dp", "blk"),
        P(None, "dp", "blk"),
        P("dp", None),
        P(),
        P(None, "dp", "blk"),
        P(None, "dp", "blk"),
    )
    out_specs = (P(None, "dp", "blk"), P(None, "dp", "blk"))
    return jax.shard_map(
        functools.partial(per_device, None),
        mesh=mesh,
        in_specs=in_specs,
        out_specs=out_specs,
        check_vma=False,
    )
```

time: 220 us -> 86 us (0.39)
  blocking collectives: 98.5 us -> 0 us
  Pallas kernels: 0 us -> 79.3 us
  waiting for transfers between devices: 50.9 us -> 0 us
  matrix products: 31.7 us -> 0 us
  starting transfers between devices: 15.8 us -> 0 us
  other arithmetic: 13.4 us -> 1.93 us
  local copies, waits for them, and re-layouts: 6.77 us -> 3 us
    pallas_call x0 -> x1, Pallas kernels: none -> 79.3 us  [per_device(): pl.pallas_call(functools.partial(kernel, cfg), out_shape=jax.ShapeDtypeSt...]
    all_to_all x2 -> x0, blocking collectives: 51.1 us -> none  [the longest x1 31.5 us: sum_at_owner(): lax.all_to_all(in_blocks(shard, dim, devices), axis, 0, 0, tiled=True)]
    all_to_all x3 -> x0, waiting for transfers between devices: 50.9 us -> none  [the longest x1 28 us: sum_at_owner(): lax.all_to_all(in_blocks(shard, dim, devices), axis, 0, 0, tiled=True)]
    all_gather x1 -> x0, blocking collectives: 47.5 us -> none  [sent_together(): whole = lax.all_gather(both, axis, axis=dim, tiled=True)]
    dot_general x10 -> x0, matrix products: 31.7 us -> none  [the longest x4 13.1 us: example_grads(): jnp.einsum('etr,tf->erf', weighted, broad, precision=lax.Precision.HIGHES...]
    all_to_all x3 -> x0, starting transfers between devices: 15.8 us -> none  [the longest x2 11.4 us: copy_for_each(): return lax.all_to_all(copies, axis, split_axis=0, concat_axis=0, tiled=True)]
    reduce_sum x5 -> x0, other arithmetic: 8.14 us -> none  [the longest x1 6.52 us: per_device(): jnp.sum(per_hidden * per_hidden, axis=(0, 2, 3))]
  transfers between devices with their start and end apart: 3 -> 0, of which waited for: 3 -> 0; matrix products, arithmetic and copies ran while one was open for 0% -> 0% of each run, Pallas kernels for 0% -> 0%
where the time goes in v1:
time: 86 us; the launch traced here: 85.5 us
  Pallas kernels  79.3 us (92%)
  local copies, waits for them, and re-layouts  3 us (3%)
  other arithmetic  1.93 us (2%)
  between operations  1.31 us (2%)
    pallas_call x1, Pallas kernels, per_device(): pl.pallas_call(functools.partial(kernel, cfg), out_shape=jax.ShapeDtypeSt...  79.3 us

profile of v1, /device:TPU:1, one launch (start us, length us, event | category | flops | bytes accessed | tf_op | source)
XLA Modules:
  0.0 85.5 jit_solution(3144174093706238890)
XLA Ops:
  1.3 0.1 pad.2.clone
  1.4 0.7 reshape.16
  2.1 0.7 reshape.17
  2.8 0.7 maximum_maximum_fusion.row_ref
  3.5 0.0 copy-start
  3.5 0.0 copy-start.1
  3.5 79.3 %clipped_step.1 = f32[72,128]{1,0:T(8,128)} custom-call(s32[1]{0:T(128)S(6)} %copy.14.thr_ref, s32[1,288]{1,0:T(1,128)} %ids_ref.1, bf16[80,128]{1,0:T(8,128)(2,1)} %maximum_maximum_fusion.row_ref, bf16[288,1024]{1,0:T(8,128)(2,1)} %a0.1, bf16[288,3328]{1,0:T(8,128)(2,1)} %a1.1, bf16[288,3328]{1,0:T(8,128)(2,1)} %a2.1, bf16[288,1024]{1,0:T(8,128)(2,1)} %a3.1), custom_call_target="tpu_custom_call" | custom-call | tf_op jit(solution)/shard_map/clipped_step/pallas_call | solution.py:445
  82.8 0.7 slice.6
  83.5 0.8 slice.7
  84.3 0.0 copy-done
  84.3 0.6 add.7
  84.9 0.0 copy-done.1
  84.9 0.6 add.6
  (2 shorter events, 0.0 us)
Async XLA Ops:
  3.5 80.8 %copy-start = (f32[2,1,3328]{2,1,0:T(1,128)S(1)}, f32[2,1,3328]{2,1,0:T(1,128)}, u32[]{:S(2)}) copy-start(f32[2,1,3328]{2,1,0:T(1,128)} %param.19) | copy-start | bytes 79876
  3.5 81.4 %copy-start.1 = (f32[2,1,1024]{2,1,0:T(1,128)S(1)}, f32[2,1,1024]{2,1,0:T(1,128)}, u32[]{:S(2)}) copy-start(f32[2,1,1024]{2,1,0:T(1,128)} %param.18) | copy-start | bytes 24580

commit v2 on v1

v2 whole, which is shorter than its diff:
```python
import functools
import math

import jax
import jax.numpy as jnp
from jax import lax
from jax.experimental import pallas as pl
from jax.experimental.pallas import tpu as pltpu
from jax.sharding import PartitionSpec as P

EX = 8
LANES = 128
SLOT = 32
DP_AXES = {32: (4, 4, 2), 4: (2, 1, 2), 8: (2, 2, 2), 16: (2, 4, 2)}
BLK_AXES = {16: (4, 4), 4: (2, 2), 2: (1, 2), 1: (1, 1)}
PAIR = (1, 0, 3, 2)
BAND = 48
F32 = jnp.float32
BF16 = jnp.bfloat16


def nt(a, b):
    return lax.dot_general(a, b, (((1,), (1,)), ((), ())), preferred_element_type=F32)


def nn(a, b):
    return lax.dot_general(a, b, (((1,), (0,)), ((), ())), preferred_element_type=F32)


def split(a):
    high = a.astype(BF16)
    return high, (a - high.astype(F32)).astype(BF16)


def remote(src, dst, send, recv, **where):
    return pltpu.make_async_remote_copy(
        src_ref=src,
        dst_ref=dst,
        send_sem=send,
        recv_sem=recv,
        device_id=where,
        device_id_type=pl.DeviceIdType.MESH,
    )


def kernel(
    cfg,
    thr_ref,
    ids_ref,
    model_ref,
    hidden_ref,
    a0,
    a1,
    a2,
    a3,
    model_out,
    hidden_out,
    wide,
    row_f32,
    row_ref,
    rows_in,
    rows_f32,
    factors,
    gram,
    gram_in,
    gram_hi,
    gram_lo,
    part,
    part_in,
    quarter,
    quarter_in,
    proj,
    plane,
    ring,
    left,
    singles,
    grads,
    pair_in,
    pair_sum,
    y_in,
    z_out,
    z_in,
    load_sem,
    row_send,
    row_recv,
    gram_send,
    gram_recv,
    part_send,
    part_recv,
    quarter_send,
    quarter_recv,
    proj_send,
    proj_recv,
    plane_send,
    plane_recv,
    ring_send,
    ring_recv,
    pair_send,
    pair_recv,
    y_send,
    y_recv,
    z_send,
    z_recv,
    token,
):
    NZL, NY, NC, NX, NZH, widths, block = cfg
    tokens = wide.shape[0]
    ranks = NZL * NY * NC
    dp, blk = lax.axis_index("dp"), lax.axis_index("blk")
    zl, y, c = dp // (NY * NC), (dp // NC) % NY, dp % NC
    x, zh = blk // NZH, blk % NZH
    nz, npl = NZL * NZH, NX * NY * NC
    zz = zh * NZL + zl
    pp = (x * NY + y) * NC + c
    zls = [lax.rem(zl + k, NZL) for k in range(NZL)]
    zhs = [lax.rem(zh + k, NZH) for k in range(NZH)]
    xs = [lax.rem(x + k, NX) for k in range(NX)]
    ys = [lax.rem(y + k, NY) for k in range(NY)]
    cs = [c, 1 - c]

    def dp_of(z_, y_, c_):
        return (z_ * NY + y_) * NC + c_

    def slot_of(z_, y_, c_):
        return (c_ * NZL + z_) * NY + y_

    def signal(semaphore, **where):
        pl.semaphore_signal(
            semaphore, inc=1, device_id=where, device_id_type=pl.DeviceIdType.MESH
        )

    def signal_along(semaphore, distance):
        for k in (distance % nz, -distance % nz):
            q = lax.rem(zz + k, nz)
            q_hi = q // NZL
            signal(semaphore, dp=dp_of(q - q_hi * NZL, y, c), blk=x * NZH + q_hi)

    offsets = [sum(widths[:i]) for i in range(4)]
    loads = []
    for i, ref in enumerate((a0, a1, a2, a3)):
        copy = pltpu.make_async_copy(
            ref, wide.at[:, pl.ds(offsets[i], widths[i])], load_sem.at[i]
        )
        copy.start()
        loads.append(copy)

    barrier = pltpu.get_barrier_semaphore()

    for k in range(1, NZL):
        signal(barrier, dp=dp_of(zls[k], y, c))
    for k in range(1, NY):
        signal(barrier, dp=dp_of(zl, ys[k], c))
    for k in range(1, NX):
        signal(barrier, blk=xs[k] * NZH + zh)
    signal(barrier, dp=dp_of(zl, y, 1 - c))
    signal_along(barrier, 2)

    row_f32[...] = jnp.zeros_like(row_f32)
    at = 0
    for ref in (model_ref, hidden_ref):
        for k in range(2):
            for j in range(ref.shape[1] // LANES):
                row_f32[at : at + 1, :] = ref[k : k + 1, j * LANES : (j + 1) * LANES].astype(F32)
                at += 1
    row_ref[...] = row_f32[...].astype(BF16)

    half, reach = tokens // 2, 256
    member_t = (
        jnp.broadcast_to(ids_ref[...], (LANES, tokens))
        == lax.broadcasted_iota(jnp.int32, (LANES, tokens), 0)
    ).astype(F32).astype(BF16)
    eye = (
        lax.broadcasted_iota(jnp.int32, (tokens, tokens), 0)
        == lax.broadcasted_iota(jnp.int32, (tokens, tokens), 1)
    ).astype(F32).astype(BF16)
    member = nt(eye, member_t)
    member_b = member.astype(BF16)
    starts = (0, tokens - reach)
    factors[...] = jnp.zeros_like(factors)

    count = 4 // NX
    tiles = tokens // BAND
    band = [min(b * BAND, tokens - LANES) for b in range(tiles)]
    for i in (0, 3, 1, 2):
        loads[i].wait()
        for b in range(2):
            total = jnp.zeros((half, reach), F32)
            for k in range(0, widths[i], 256):
                n = min(256, widths[i] - k)
                at = offsets[i] + k
                total += nt(
                    wide[b * half : (b + 1) * half, at : at + n],
                    wide[starts[b] : starts[b] + reach, at : at + n],
                )
            for tile in range(b * tiles // 2, (b + 1) * tiles // 2):
                down = tile * BAND - b * half
                right = band[tile] - starts[b]
                gram[PAIR[i] // count, PAIR[i] % count, tile] = total[
                    down : down + BAND, right : right + LANES
                ]

    pl.semaphore_wait(barrier, NZL + NY + NX)
    signal_along(token.at[0], 2)

    own = slot_of(zl, y, c)
    sends = []

    def row_copy(src, slot, where):
        copy = remote(src, rows_in.at[slot], row_send.at[len(sends)], row_recv.at[slot], dp=where)
        copy.start()
        sends.append(copy)

    def row_wait(slot):
        remote(
            rows_in.at[slot], rows_in.at[slot], row_send.at[0], row_recv.at[slot], dp=dp_of(zl, y, 1 - c)
        ).wait_recv()

    for k in range(1, NZL):
        row_copy(row_ref, own, dp_of(zls[k], y, c))
    for j in range(1, NY):
        row_copy(row_ref, own, dp_of(zl, ys[j], c))
    row_copy(row_ref, own, dp_of(zl, y, 1 - c))
    gram_copies = []
    for k in range(1, NX):
        copy = remote(
            gram.at[xs[k]], gram_in.at[x], gram_send.at[k], gram_recv.at[k], blk=xs[k] * NZH + zh
        )
        copy.start()
        gram_copies.append(copy)

    for k in range(1, NZL):
        z_ = zls[k]
        slot = slot_of(z_, y, c)
        row_wait(slot)
        for j in range(1, NY):
            row_copy(rows_in.at[slot], slot, dp_of(zl, ys[j], c))
        row_copy(rows_in.at[slot], slot, dp_of(zl, y, 1 - c))
    for k in range(NZL):
        for j in range(1, NY):
            slot = slot_of(zls[k], ys[j], c)
            row_wait(slot)
            row_copy(rows_in.at[slot], slot, dp_of(zl, y, 1 - c))

    pl.semaphore_wait(token.at[0], 2)
    signal_along(token.at[1], 4)

    def widen(ref, slot):
        at = pl.multiple_of(slot * block, 8)
        rows_f32[pl.ds(at, block), :] = ref[...].astype(F32)[:block]

    widen(row_ref, own)
    for k in range(NZL):
        for j in range(NY):
            if k or j:
                slot = slot_of(zls[k], ys[j], c)
                widen(rows_in.at[slot], slot)
    for k in range(NZL):
        for j in range(NY):
            slot = slot_of(zls[k], ys[j], 1 - c)
            row_wait(slot)
            widen(rows_in.at[slot], slot)

    chunks = [w // LANES for w in widths]
    firsts = (0, chunks[0] + chunks[3], chunks[0] + chunks[3] + chunks[1], chunks[0])
    for i in range(4):
        for j in range(chunks[i]):
            picked = rows_f32[pl.ds(firsts[i] + j, ranks, stride=block), :]
            at = offsets[i] + j * LANES
            factors[SLOT * i : SLOT * i + ranks, at : at + LANES] = picked.astype(BF16)

    total = jnp.zeros((tokens, LANES), F32)
    for k in range(0, wide.shape[1], 256):
        n = min(256, wide.shape[1] - k)
        total += nt(wide[:, k : k + n], factors[:, k : k + n])
    lane = lax.broadcasted_iota(jnp.int32, (tokens // 4, LANES), 1) // SLOT
    for q in range(4):
        packed = jnp.zeros((tokens // 4, LANES), F32)
        for g in range(4):
            piece = total[g * tokens // 4 : (g + 1) * tokens // 4]
            if g != q:
                piece = pltpu.roll(piece, SLOT * (g - q) % LANES, 1)
            packed = jnp.where(lane == g, piece, packed)
        part[q // count, q % count] = packed

    copies = []
    for k in range(1, NX):
        x_ = xs[k]
        copy = remote(
            part.at[x_], part_in.at[x], part_send.at[k], part_recv.at[k], blk=x_ * NZH + zh
        )
        copy.start()
        copies.append(copy)
    for copy in gram_copies:
        copy.wait_recv()
    sends += gram_copies
    for tile in range(tiles):
        own_at = tile * BAND
        same = nt(member_b[own_at : own_at + BAND], member_b[band[tile] : band[tile] + LANES])
        ahead = (
            band[tile]
            - own_at
            + lax.broadcasted_iota(jnp.int32, (BAND, LANES), 1)
            - lax.broadcasted_iota(jnp.int32, (BAND, LANES), 0)
        )
        times = jnp.where(ahead > 0, 2.0, jnp.where(ahead == 0, 1.0, 0.0)) * same
        for q in range(count):
            total = gram[x, q, tile]
            for k in range(1, NX):
                total += gram_in[xs[k], q, tile]
            high, low = split(times * total)
            gram_hi[q, tile] = high
            gram_lo[q, tile] = low
    for copy in copies:
        copy.wait_recv()
    pl.semaphore_wait(token.at[1], 2)
    held = part[x]
    for k in range(1, NX):
        held += part_in[xs[k]]
    quarter[...] = held
    sends += copies
    copies = []
    for k in range(1, NZH):
        copy = remote(
            quarter,
            quarter_in.at[zh],
            quarter_send.at[k],
            quarter_recv.at[k],
            blk=x * NZH + zhs[k],
        )
        copy.start()
        copies.append(copy)
    for copy in copies:
        copy.wait_recv()
    for k in range(1, NZH):
        held += quarter_in[zhs[k]]
    proj[x] = held
    sends += copies
    copies = []
    for k in range(1, NX):
        copy = remote(
            proj.at[x], proj.at[x], proj_send.at[k], proj_recv.at[k], blk=(xs[k]) * NZH + zh
        )
        copy.start()
        copies.append(copy)

    norm = jnp.zeros((1, LANES), F32)
    for q in range(count):
        mine = jnp.concatenate(
            [
                jnp.where(lane == 0, held[q] if g == 0 else pltpu.roll(held[q], LANES - SLOT * g, 1), 0.0)
                for g in range(4)
            ],
            axis=0,
        )
        high = mine.astype(BF16).astype(F32)
        both = (high + pltpu.roll(mine - high, SLOT, 1)).astype(BF16)
        for tile in range(tiles):
            near = both[band[tile] : band[tile] + LANES]
            mixed = nn(gram_hi[q, tile], near) + nn(gram_lo[q, tile], near)
            mixed += pltpu.roll(mixed, LANES - SLOT, 1)
            own_at = tile * BAND
            each = jnp.sum(mixed * mine[own_at : own_at + BAND], axis=1, keepdims=True)
            norm += jnp.sum(member[own_at : own_at + BAND] * each, axis=0, keepdims=True)

    plane[pp] = norm

    for k in range(NX):
        for j in range(NY):
            for i in range(NC):
                if k or j or i:
                    remote(
                        plane.at[pp],
                        plane.at[pp],
                        plane_send,
                        plane_recv,
                        dp=dp_of(zl, ys[j], cs[i]),
                        blk=xs[k] * NZH + zh,
                    ).start()

    for copy in copies:
        copy.wait_recv()
    sends += copies
    pieces = []
    for g in range(4):
        piece = jnp.zeros((tokens // 4, LANES), F32)
        for q in range(4):
            packed = proj[q // count, q % count]
            if g != q:
                packed = pltpu.roll(packed, SLOT * (q - g) % LANES, 1)
            piece = jnp.where(lane == q, packed, piece)
        pieces.append(piece)
    high, low = split(jnp.concatenate(pieces, axis=0))
    eye = (
        lax.broadcasted_iota(jnp.int32, (LANES, LANES), 0)
        == lax.broadcasted_iota(jnp.int32, (LANES, LANES), 1)
    ).astype(F32).astype(BF16)
    high_t, low_t = nt(eye, high), nt(eye, low)
    for e in range(EX):
        here = jnp.broadcast_to(ids_ref[...], (SLOT, tokens)) == e
        for i in range(4):
            at = SLOT * PAIR[i]
            for n, part_t in enumerate((high_t, low_t)):
                left[i, (2 * e + n) * SLOT : (2 * e + n + 1) * SLOT] = jnp.where(
                    here, part_t[at : at + SLOT], 0.0
                ).astype(BF16)

    rest = plane.at[pl.ds(0, npl - 1)]
    remote(rest, rest, plane_send, plane_recv, dp=dp_of(zl, y, 1 - c)).wait()
    everyone = jnp.sum(plane[...], axis=0)
    group = jnp.zeros((1, LANES), F32)
    for k in range(NX):
        group += plane[(k * NY + y) * NC + c]
    ring[zz] = jnp.concatenate([group, everyone], axis=0)

    for k in sorted(range(NZH), key=lambda d: -min(d, NZH - d)):
        for j in range(NZL):
            if k or j:
                remote(
                    ring.at[zz],
                    ring.at[zz],
                    ring_send,
                    ring_recv,
                    dp=dp_of(zls[j], y, c),
                    blk=x * NZH + zhs[k],
                ).start()

    for i in range(4):
        step = 256 if widths[i] % 256 == 0 else LANES
        for k in range(0, widths[i], step):
            at = offsets[i] + k
            got = nn(left[i], wide[:, at : at + step]).reshape(EX, 2, SLOT // 8, 8, step)
            singles[:, :, :, at : at + step] = got[:, 0] + got[:, 1]

    rest = ring.at[pl.ds(0, nz - 1)]
    remote(rest, rest, ring_send, ring_recv, dp=dp_of(zl, y, 1 - c)).wait()
    everyone = jnp.sum(ring[...], axis=0)[1:2]
    group = jnp.zeros((1, LANES), F32)
    for k in range(NZH):
        group += ring[k * NZL + zl][0:1]
    grand_total = jnp.sum(everyone, axis=1, keepdims=True)
    root_mean = jnp.sqrt(jnp.maximum(grand_total, 0.0) / (ranks * EX) + 1e-06)
    clip = (0.5 + 0.125 * thr_ref[...].astype(F32)) * root_mean
    factor = jnp.minimum(1.0, clip * lax.rsqrt(jnp.maximum(group, 0.0) + 1e-06))
    entries = 2 * ranks * NX * NZH * (widths[0] + widths[1])
    rescale = math.sqrt(entries / (ranks * EX)) / clip
    scaled = factor * rescale
    lane = lax.broadcasted_iota(jnp.int32, (1, LANES), 1)
    weights = [
        jnp.broadcast_to(
            jnp.sum(jnp.where(lane == e, scaled, 0.0), axis=1, keepdims=True), (8, LANES)
        )
        for e in range(EX)
    ]

    def clipped(g):
        for i in range(4):
            for j in range(chunks[i]):
                at = offsets[i] + j * LANES
                total = weights[0] * singles[0, g, :, at : at + LANES]
                for e in range(1, EX):
                    total += weights[e] * singles[e, g, :, at : at + LANES]
                grads[pl.ds(g * (8 * block) + firsts[i] + j, 8, stride=block), :] = total

    wide_block = NY * block
    groups = NZL * NY // 8
    if groups == 2:
        pair_at = zl // 2
        away = 2 * lax.rem(pair_at + 1, 2)
        other = 2 * pair_at + 1 - lax.rem(zl, 2)
        order = [away, away + 1, other, zl]
        sets = [lax.rem(pair_at + 1, 2), pair_at]
    else:
        order = [1 - zl, zl]
        sets = [0] * groups
        if not groups:
            for g in range(-(-ranks // 8)):
                clipped(g)
    batch = len(order) // max(groups, 1)
    copies = []
    for n in range(max(groups, 1)):
        if groups:
            clipped((1 - c) * groups + sets[n])
        for o in range(n * batch, (n + 1) * batch):
            at = pl.multiple_of(((1 - c) * NZL + order[o]) * wide_block, 8)
            copy = remote(
                grads.at[pl.ds(at, wide_block)],
                pair_in.at[o],
                pair_send.at[o],
                pair_recv.at[o],
                dp=dp_of(zl, y, 1 - c),
            )
            copy.start()
            copies.append(copy)
    sends += copies
    y_copies = {}
    for n in range(max(groups, 1)):
        if groups:
            clipped(c * groups + sets[n])
        for o in range(n * batch, (n + 1) * batch):
            at = pl.multiple_of((c * NZL + order[o]) * wide_block, 8)
            copies[o].wait_recv()
            pair_sum[o] = (grads[pl.ds(at, wide_block), :] + pair_in[o]).reshape(NY, block, LANES)
            for j in range(1, NY):
                copy = remote(
                    pair_sum.at[o, ys[j]],
                    y_in.at[o, y],
                    y_send.at[o, j],
                    y_recv.at[o, j],
                    dp=dp_of(zl, ys[j], c),
                )
                copy.start()
                y_copies[o, j] = copy
    last = NZL - 1
    for o in range(NZL):
        held = pair_sum[o, y]
        for j in range(1, NY):
            y_copies[o, j].wait_recv()
            sends.append(y_copies[o, j])
        for j in range(1, NY):
            held += y_in[o, ys[j]]
        if o < last:
            z_out[o] = held
            copy = remote(
                z_out.at[o], z_in.at[zl], z_send.at[o], z_recv.at[zl], dp=dp_of(order[o], y, c)
            )
            copy.start()
            sends.append(copy)
    for k in range(1, NZL):
        remote(
            z_in.at[zls[k]], z_in.at[zls[k]], z_send.at[0], z_recv.at[zls[k]], dp=dp_of(zl, y, 1 - c)
        ).wait_recv()
    for k in range(1, NZL):
        held += z_in[zls[k]]
    row_f32[: held.shape[0], :] = held
    at = 0
    for ref in (model_out, hidden_out):
        for k in range(2):
            for j in range(ref.shape[2] // LANES):
                ref[k, :, j * LANES : (j + 1) * LANES] = row_f32[at : at + 1, :]
                at += 1
    for copy in sends:
        copy.wait_send()


def per_device(
    block_input_rows,
    up_loss_gradient,
    down_projection_input,
    output_loss_gradient,
    model_side_factors,
    hidden_side_factors,
    example_index_rows,
    clipping_threshold,
    model_side_noise,
    hidden_side_noise,
):
    ndp, nblk = lax.axis_size("dp"), lax.axis_size("blk")
    NZL, NY, NC = DP_AXES[ndp]
    NX, NZH = BLK_AXES[nblk]
    tokens = block_input_rows.shape[0]
    model, hidden = block_input_rows.shape[1], up_loss_gradient.shape[1]
    widths = (model, hidden, hidden, model)
    total = sum(widths)
    rows = total // LANES
    block = -(-rows // 8) * 8
    sent = -(-rows // 16) * 16
    cfg = (NZL, NY, NC, NX, NZH, widths, block)
    count, tiles = 4 // NX, tokens // BAND
    dma = pltpu.SemaphoreType.DMA
    vmem = pl.BlockSpec(memory_space=pltpu.VMEM)
    hbm = pl.BlockSpec(memory_space=pl.ANY)
    summed = pl.pallas_call(
        functools.partial(kernel, cfg),
        out_shape=[
            jax.ShapeDtypeStruct(model_side_noise.shape, F32),
            jax.ShapeDtypeStruct(hidden_side_noise.shape, F32),
        ],
        in_specs=[vmem, vmem, vmem, vmem, hbm, hbm, hbm, hbm],
        out_specs=[vmem, vmem],
        scratch_shapes=[
            pltpu.VMEM((tokens, total), BF16),
            pltpu.VMEM((sent, LANES), F32),
            pltpu.VMEM((sent, LANES), BF16),
            pltpu.VMEM((ndp, sent, LANES), BF16),
            pltpu.VMEM((ndp * block, LANES), F32),
            pltpu.VMEM((LANES, total), BF16),
            pltpu.VMEM((NX, count, tiles, BAND, LANES), F32),
            pltpu.VMEM((NX, count, tiles, BAND, LANES), F32),
            pltpu.VMEM((count, tiles, BAND, LANES), BF16),
            pltpu.VMEM((count, tiles, BAND, LANES), BF16),
            pltpu.VMEM((NX, count, tokens // 4, LANES), F32),
            pltpu.VMEM((NX, count, tokens // 4, LANES), F32),
            pltpu.VMEM((count, tokens // 4, LANES), F32),
            pltpu.VMEM((NZH, count, tokens // 4, LANES), F32),
            pltpu.VMEM((NX, count, tokens // 4, LANES), F32),
            pltpu.VMEM((NX * NY * NC, 1, LANES), F32),
            pltpu.VMEM((NZL * NZH, 2, LANES), F32),
            pltpu.VMEM((4, 2 * EX * SLOT, tokens), BF16),
            pltpu.VMEM((EX, SLOT // 8, 8, total), F32),
            pltpu.VMEM((ndp * block, LANES), F32),
            pltpu.VMEM((NZL, NY * block, LANES), F32),
            pltpu.VMEM((NZL, NY, block, LANES), F32),
            pltpu.VMEM((NZL, NY, block, LANES), F32),
            pltpu.VMEM((NZL, block, LANES), F32),
            pltpu.VMEM((NZL, block, LANES), F32),
            dma((4,)),
            dma((ndp,)),
            dma((ndp,)),
            dma((NX,)),
            dma((NX,)),
            dma((NX,)),
            dma((NX,)),
            dma((NZH,)),
            dma((NZH,)),
            dma((NX,)),
            dma((NX,)),
            dma,
            dma,
            dma,
            dma,
            dma((NZL,)),
            dma((NZL,)),
            dma((NZL, NY)),
            dma((NZL, NY)),
            dma((NZL,)),
            dma((NZL,)),
            pltpu.SemaphoreType.REGULAR((2,)),
        ],
        compiler_params=pltpu.CompilerParams(
            collective_id=0, has_side_effects=True, vmem_limit_bytes=56 << 20
        ),
        name="clipped_step",
    )(
        clipping_threshold.reshape(1, 1),
        example_index_rows,
        model_side_factors.reshape(2, model),
        hidden_side_factors.reshape(2, hidden),
        block_input_rows,
        up_loss_gradient,
        down_projection_input,
        output_loss_gradient,
    )
    return (summed[0] + model_side_noise, summed[1] + hidden_side_noise)


def solution(mesh):
    in_specs = (
        P("dp", "blk"),
        P("dp", "blk"),
        P("dp", "blk"),
        P("dp", "blk"),
        P(None, "dp", "blk"),
        P(None, "dp", "blk"),
        P("dp", None),
        P(),
        P(None, "dp", "blk"),
        P(None, "dp", "blk"),
    )
    out_specs = (P(None, "dp", "blk"), P(None, "dp", "blk"))
    return jax.shard_map(
        per_device,
        mesh=mesh,
        in_specs=in_specs,
        out_specs=out_specs,
        check_vma=False,
    )
```

time: 86 us -> 74.7 us (0.87)
  Pallas kernels: 79.3 us -> 70.4 us
  local copies, waits for them, and re-layouts: 3 us -> 0.01 us
    pallas_call x1, Pallas kernels: 79.3 us -> 70.4 us  [per_device(): pl.pallas_call(functools.partial(kernel, cfg), out_shape=[jax.ShapeDtypeS...]
    reshape x3 -> x0, local copies, waits for them, and re-layouts: 1.46 us -> none  [the longest x1 0.74 us: per_device(): hidden_side_factors.reshape(-1, LANES)]
    slice x2 -> x0, local copies, waits for them, and re-layouts: 1.45 us -> none  [the longest x1 0.75 us: per_device(): summed[cut:rows].reshape(hidden_side_noise.shape) + hidden_side_noise]
    add x2, other arithmetic: 1.25 us -> 2.69 us  [per_device(): return (summed[0] + model_side_noise, summed[1] + hidden_side_noise)]
where the time goes in v2:
time: 74.7 us; the launch traced here: 74.4 us
  Pallas kernels  70.4 us (94%)
  other arithmetic  2.69 us (4%)
  between operations  1.31 us (2%)
    pallas_call x1, Pallas kernels, per_device(): pl.pallas_call(functools.partial(kernel, cfg), out_shape=[jax.ShapeDtypeS...  70.4 us
    add x2, other arithmetic, per_device(): return (summed[0] + model_side_noise, summed[1] + hidden_side_noise)  2.69 us

profile of v2, /device:TPU:1, one launch (start us, length us, event | category | flops | bytes accessed | tf_op | source)
XLA Modules:
  0.0 74.4 jit_solution(11979300572743966389)
XLA Ops:
  1.3 0.0 copy-start.1
  1.3 0.0 copy-start
  1.3 70.4 %clipped_step.1 = (f32[2,1,1024]{2,1,0:T(1,128)}, f32[2,1,3328]{2,1,0:T(1,128)}) custom-call(s32[1,1]{1,0:T(1,128)} %bitcast.3.thr_ref, s32[1,288]{1,0:T(1,128)} %ids_ref.1, bf16[2,1024]{1,0:T(2,128)(2,1)} %bitcast.5, bf16[2,3328]{1,0:T(2,128)(2,1)} %bitcast.4, bf16[288,1024]{1,0:T(8,128)(2,1)} %a0.1, bf16[288,3328]{1,0:T(8,128)(2,1)} %a1.1, ...), custom_call_target="tpu_custom_call" | custom-call | tf_op jit(solution)/shard_map/clipped_step/pallas_call | solution.py:572
  71.7 0.0 copy-done.1
  71.7 1.3 %add.6 = f32[2,1,1024]{2,1,0:T(1,128)} add(f32[2,1,1024]{2,1,0:T(1,128)} %get-tuple-element.4, f32[2,1,1024]{2,1,0:T(1,128)S(1)} %copy-done.1) | non-fusion elementwise | flops 2048 | bytes 24576 | tf_op jit(solution)/shard_map/add | solution.py:643
  73.0 0.0 copy-done
  73.0 1.4 %add.7 = f32[2,1,3328]{2,1,0:T(1,128)} add(f32[2,1,3328]{2,1,0:T(1,128)} %get-tuple-element.5, f32[2,1,3328]{2,1,0:T(1,128)S(1)} %copy-done) | non-fusion elementwise | flops 6656 | bytes 79872 | tf_op jit(solution)/shard_map/add | solution.py:643
Async XLA Ops:
  1.3 70.4 %copy-start.1 = (f32[2,1,1024]{2,1,0:T(1,128)S(1)}, f32[2,1,1024]{2,1,0:T(1,128)}, u32[]{:S(2)}) copy-start(f32[2,1,1024]{2,1,0:T(1,128)} %param.18) | copy-start | bytes 24580
  1.3 71.7 %copy-start = (f32[2,1,3328]{2,1,0:T(1,128)S(1)}, f32[2,1,3328]{2,1,0:T(1,128)}, u32[]{:S(2)}) copy-start(f32[2,1,3328]{2,1,0:T(1,128)} %param.19) | copy-start | bytes 79876

commit v3 on v2

--- a/solution.py
+++ b/solution.py
@@ -404,6 +404,23 @@
                     here, part_t[at : at + SLOT], 0.0
                 ).astype(BF16)
 
+    reached = reach // 72
+    cut = reached * 2 * SLOT
+
+    def examples_of(arrays):
+        for i in arrays:
+            step = 256 if widths[i] % 256 == 0 else LANES
+            for k in range(0, widths[i], step):
+                across = slice(offsets[i] + k, offsets[i] + k + step)
+                early = nn(left[i, :cut, :reach], wide[:reach, across])
+                early = early.reshape(reached, 2, SLOT // 8, 8, step)
+                singles[:reached, :, :, across] = early[:, 0] + early[:, 1]
+                later = nn(left[i, cut:], wide[:, across])
+                later = later.reshape(EX - reached, 2, SLOT // 8, 8, step)
+                singles[reached:, :, :, across] = later[:, 0] + later[:, 1]
+
+    examples_of((0, 3))
+
     rest = plane.at[pl.ds(0, npl - 1)]
     remote(rest, rest, plane_send, plane_recv, dp=dp_of(zl, y, 1 - c)).wait()
     everyone = jnp.sum(plane[...], axis=0)
@@ -424,12 +441,7 @@
                     blk=x * NZH + zhs[k],
                 ).start()
 
-    for i in range(4):
-        step = 256 if widths[i] % 256 == 0 else LANES
-        for k in range(0, widths[i], step):
-            at = offsets[i] + k
-            got = nn(left[i], wide[:, at : at + step]).reshape(EX, 2, SLOT // 8, 8, step)
-            singles[:, :, :, at : at + step] = got[:, 0] + got[:, 1]
+    examples_of((1, 2))
 
     rest = ring.at[pl.ds(0, nz - 1)]
     remote(rest, rest, ring_send, ring_recv, dp=dp_of(zl, y, 1 - c)).wait()

time: 74.7 us -> 74.1 us (level)
  no operation moved by 1% of the time
where the time goes in v3:
time: 74.1 us; the launch traced here: 73.7 us
  Pallas kernels  69.7 us (94%)
  other arithmetic  2.69 us (4%)
  between operations  1.31 us (2%)
    pallas_call x1, Pallas kernels, per_device(): pl.pallas_call(functools.partial(kernel, cfg), out_shape=[jax.ShapeDtypeS...  69.7 us
    add x2, other arithmetic, per_device(): return (summed[0] + model_side_noise, summed[1] + hidden_side_noise)  2.69 us

profile of v3, /device:TPU:1, one launch (start us, length us, event | category | flops | bytes accessed | tf_op | source)
XLA Modules:
  0.0 73.7 jit_solution(4394995619652947322)
XLA Ops:
  1.3 0.0 copy-start.1
  1.3 0.0 copy-start
  1.3 69.7 %clipped_step.1 = (f32[2,1,1024]{2,1,0:T(1,128)}, f32[2,1,3328]{2,1,0:T(1,128)}) custom-call(s32[1,1]{1,0:T(1,128)} %bitcast.3.thr_ref, s32[1,288]{1,0:T(1,128)} %ids_ref.1, bf16[2,1024]{1,0:T(2,128)(2,1)} %bitcast.5, bf16[2,3328]{1,0:T(2,128)(2,1)} %bitcast.4, bf16[288,1024]{1,0:T(8,128)(2,1)} %a0.1, bf16[288,3328]{1,0:T(8,128)(2,1)} %a1.1, ...), custom_call_target="tpu_custom_call" | custom-call | tf_op jit(solution)/shard_map/clipped_step/pallas_call | solution.py:584
  71.0 0.0 copy-done.1
  71.0 1.3 %add.6 = f32[2,1,1024]{2,1,0:T(1,128)} add(f32[2,1,1024]{2,1,0:T(1,128)} %get-tuple-element.4, f32[2,1,1024]{2,1,0:T(1,128)S(1)} %copy-done.1) | non-fusion elementwise | flops 2048 | bytes 24576 | tf_op jit(solution)/shard_map/add | solution.py:655
  72.3 0.0 copy-done
  72.4 1.4 %add.7 = f32[2,1,3328]{2,1,0:T(1,128)} add(f32[2,1,3328]{2,1,0:T(1,128)} %get-tuple-element.5, f32[2,1,3328]{2,1,0:T(1,128)S(1)} %copy-done) | non-fusion elementwise | flops 6656 | bytes 79872 | tf_op jit(solution)/shard_map/add | solution.py:655
Async XLA Ops:
  1.3 69.8 %copy-start.1 = (f32[2,1,1024]{2,1,0:T(1,128)S(1)}, f32[2,1,1024]{2,1,0:T(1,128)}, u32[]{:S(2)}) copy-start(f32[2,1,1024]{2,1,0:T(1,128)} %param.18) | copy-start | bytes 24580
  1.3 71.1 %copy-start = (f32[2,1,3328]{2,1,0:T(1,128)S(1)}, f32[2,1,3328]{2,1,0:T(1,128)}, u32[]{:S(2)}) copy-start(f32[2,1,3328]{2,1,0:T(1,128)} %param.19) | copy-start | bytes 79876
